TPU v7x, 32 devices: a whole 2x2x4 slice. The times are simulated.
32 devices in a mesh: tm: 32 (over z, y, x, core).
Axes of the slice: x: 2, y: 2, z: 4, core: 2. Of those that a mesh axis runs over, the one named last changes fastest.
Arguments:
- samples: int32 [65536, 128], P('tm'), may hold values from -8 to 7
Outputs:
- spectra: float32 [2, 128, 16384], P(None, None, 'tm')
All inputs are finite; a program needn't handle non-finite values.
Results may differ from a plain program's by a relative error of at most 0.0003.
Values may be sent and summed in bfloat16 or wider, within the bound.
A program may use at most 192 MiB of HBM per device.

v0:
```python
import functools

import jax
import jax.numpy as jnp
import numpy as np
from jax import lax
from jax.experimental import pallas as pl
from jax.experimental.pallas import tpu as pltpu
from jax.sharding import PartitionSpec as P

LAGS = 128
Q = 16
JS = 16
TAUS = LAGS + Q
OUT_ROWS = (LAGS + 1) * JS
TILE = OUT_ROWS // 3
MESH = pl.DeviceIdType.MESH


def flipped(value, mask):
    out = 0
    bit = 1
    while bit <= 64:
        b = (value // bit) % 2
        out = out + ((b + (1 if mask & bit else 0)) % 2) * bit
        bit *= 2
    return out


def kernel(n, T, G, mj, iw, samples, perm, out, vbuf, ts, tb, ut, acc, sbuf, rbuf,
           send_v, recv_v, send_t, recv_t, send_h, send_r, recv_r):
    me = lax.axis_index("tm")
    g = me % G
    t = me // G
    core = g % 2
    base = t * G
    rows = samples.shape[0]
    R = rows // Q
    C = G // 2

    for q in range(Q):
        phase = samples[pl.ds(q, R, stride=Q), :].astype(jnp.float32).astype(jnp.bfloat16)
        vbuf[g, q // 2, :, (q % 2) * 128:(q % 2 + 1) * 128] = phase
        turned = lax.dot_general(
            perm[...], phase, (((1,), (1,)), ((), ())), preferred_element_type=jnp.float32
        ).astype(jnp.bfloat16)
        for d in range(G):
            ts[d, q * JS:(q + 1) * JS, :] = turned[d * JS:(d + 1) * JS, :]

    def copy_t(k):
        d = flipped(g, k)
        return pltpu.make_async_remote_copy(
            src_ref=ts.at[d], dst_ref=tb.at[g], send_sem=send_t.at[k], recv_sem=recv_t.at[g],
            device_id=(base + d,), device_id_type=MESH)

    def copy_h(d):
        return pltpu.make_async_remote_copy(
            src_ref=ts.at[d], dst_ref=tb.at[G], send_sem=send_h.at[d], recv_sem=recv_t.at[G],
            device_id=(base - G + d,), device_id_type=MESH)

    def copy_v(slot, d, sem):
        return pltpu.make_async_remote_copy(
            src_ref=vbuf.at[slot], dst_ref=vbuf.at[slot], send_sem=send_v.at[sem],
            recv_sem=recv_v.at[slot], device_id=(base + d,), device_id_type=MESH)

    partner = flipped(g, 1)
    for k in range(1, G):
        copy_t(k).start()

    @pl.when(jnp.logical_and(g == 0, t > 0))
    def _():
        for d in range(G):
            copy_h(d).start()

    for c in range(1, C):
        copy_v(g, flipped(g, 2 * c), c).start()
    copy_v(g, partner, 0).start()

    tb[g] = ts[g]

    @pl.when(t == T - 1)
    def _():
        tb[G] = jnp.zeros(tb.shape[1:], tb.dtype)

    @pl.when(t < T - 1)
    def _():
        pltpu.make_async_copy(tb.at[G], tb.at[G], recv_t.at[G]).wait()

    for k in range(1, G):
        s = flipped(g, k)
        pltpu.make_async_copy(tb.at[s], tb.at[s], recv_t.at[s]).wait()

    def build(d, carry):
        pair = jnp.concatenate([tb[d], tb[d + 1]], axis=1)
        ut[d, 0:Q * JS, :] = tb[d]
        for s in range(1, TAUS // Q):
            ut[d, s * Q * JS:(s + 1) * Q * JS, :] = pair[:, s:s + R]
        return carry

    lax.fori_loop(0, G, build, 0)

    def multiply(d, first):
        weights = vbuf[d].reshape(Q // 2 * R, 256)

        def tile(i, carry):
            r0 = pl.multiple_of(i * TILE, JS)
            left = jnp.concatenate(
                [ut[d, pl.ds(pl.multiple_of(r0 + 2 * JS * e, JS), TILE), :] for e in range(Q // 2)], axis=1)
            part = jnp.dot(left, weights, preferred_element_type=jnp.float32)
            for h in range(2):
                half = part[:, h * 128:(h + 1) * 128]
                if first:
                    acc[h, pl.ds(r0, TILE), :] = half
                else:
                    acc[h, pl.ds(r0, TILE), :] += half
            return carry

        lax.fori_loop(0, OUT_ROWS // TILE, tile, 0)

    def wait_v(s):
        pltpu.make_async_copy(vbuf.at[s], vbuf.at[s], recv_v.at[s]).wait()

    multiply(g, True)
    wait_v(partner)
    multiply(partner, False)
    for c in range(1, C):
        s = flipped(g, 2 * c)
        wait_v(s)
        copy_v(s, partner, C + c - 1).start()
        multiply(s, False)
        if c > 1:
            s2 = flipped(g, 2 * (c - 1) + 1)
            wait_v(s2)
            multiply(s2, False)
    if C > 1:
        s2 = flipped(g, 2 * (C - 1) + 1)
        wait_v(s2)
        multiply(s2, False)

    def piece(j):
        full = acc[0, pl.ds(j, LAGS, stride=JS), :] + acc[1, pl.ds(JS + j, LAGS, stride=JS), :]
        if iw == 128:
            return full
        return sum(jnp.where(g % (128 // iw) == h, full[:, h * iw:(h + 1) * iw], 0.0) for h in range(128 // iw))

    def copy_r(k):
        d = (t + k) % T
        return pltpu.make_async_remote_copy(
            src_ref=sbuf.at[d], dst_ref=rbuf.at[t], send_sem=send_r.at[k], recv_sem=recv_r.at[t],
            device_id=(d * G + g,), device_id_type=MESH)

    for k in list(range(1, T)) + [0]:
        d = (t + k) % T
        for m in range(mj):
            if k:
                sbuf[d, m] = piece(d * mj + m)
            else:
                rbuf[t, m] = piece(d * mj + m)
        if k:
            copy_r(k).start()
    for k in range(1, T):
        s = (t + T - k) % T
        pltpu.make_async_copy(rbuf.at[s], rbuf.at[s], recv_r.at[s]).wait()
    for m in range(mj):
        total = rbuf[0, m]
        for k in range(1, T):
            total = total + rbuf[k, m]
        out[:, m * iw:(m + 1) * iw] = total

    for k in range(1, G):
        copy_t(k).wait_send()

    @pl.when(jnp.logical_and(g == 0, t > 0))
    def _():
        for d in range(G):
            copy_h(d).wait_send()

    for c in range(1, C):
        copy_v(g, flipped(g, 2 * c), c).wait_send()
        copy_v(flipped(g, 2 * c), partner, C + c - 1).wait_send()
    copy_v(g, partner, 0).wait_send()
    for k in range(1, T):
        copy_r(k).wait_send()


def on_device(n, samples):
    rows, width = samples.shape
    owned = width * width // n
    mj = max(1, owned // width)
    iw = min(width, owned)
    T = JS // mj
    G = n // T
    R = rows // Q
    perm = np.zeros((G * JS, width), np.float32)
    for d in range(G):
        for s in range(T):
            for m in range(mj):
                perm[d * JS + s * mj + m, (s * G + d) * owned // width + m] = 1
    lagged = pl.pallas_call(
        functools.partial(kernel, n, T, G, mj, iw),
        out_shape=jax.ShapeDtypeStruct((LAGS, owned), jnp.float32),
        in_specs=[pl.BlockSpec(memory_space=pltpu.VMEM)] * 2,
        out_specs=pl.BlockSpec(memory_space=pltpu.VMEM),
        scratch_shapes=[
            pltpu.VMEM((G, Q // 2, R, 2 * width), jnp.bfloat16),
            pltpu.VMEM((G, Q * JS, R), jnp.bfloat16),
            pltpu.VMEM((G + 1, Q * JS, R), jnp.bfloat16),
            pltpu.VMEM((G, TAUS * JS, R), jnp.bfloat16),
            pltpu.VMEM((2, OUT_ROWS, width), jnp.float32),
            pltpu.VMEM((T, mj, LAGS, iw), jnp.float32),
            pltpu.VMEM((T, mj, LAGS, iw), jnp.float32),
            pltpu.SemaphoreType.DMA((G,)),
            pltpu.SemaphoreType.DMA((G,)),
            pltpu.SemaphoreType.DMA((G,)),
            pltpu.SemaphoreType.DMA((G + 1,)),
            pltpu.SemaphoreType.DMA((G,)),
            pltpu.SemaphoreType.DMA((T,)),
            pltpu.SemaphoreType.DMA((T,)),
        ],
        compiler_params=pltpu.CompilerParams(has_side_effects=True, vmem_limit_bytes=56 * 1024 * 1024),
    )(samples, jnp.asarray(perm, jnp.bfloat16))
    k = np.arange(LAGS)
    angle = 2.0 * np.pi / LAGS * (np.outer(k, k) % LAGS)
    table = np.concatenate([np.cos(angle), -np.sin(angle)]) / (16.0 * rows * n)
    spectra = jnp.dot(
        jnp.asarray(table, jnp.float32), lagged,
        preferred_element_type=jnp.float32, precision=lax.Precision.HIGHEST)
    return spectra.reshape(2, LAGS, owned)


def solution(mesh):
    return jax.shard_map(
        functools.partial(on_device, mesh.shape["tm"]), mesh=mesh,
        in_specs=(P("tm", None),), out_specs=P(None, None, "tm"), check_vma=False)
```

profile of v0, /device:TPU:8, one launch (start us, length us, event | category | flops | bytes accessed | tf_op | source)
XLA Modules:
  0.0 72.5 jit_solution(16976730437000711736)
XLA Ops:
  0.0 0.0 copy-start
  0.0 70.1 %shard_map.37 = f32[128,512]{1,0:T(8,128)} custom-call(s32[2048,128]{1,0:T(8,128)} %samples.1, bf16[128,128]{1,0:T(8,128)(2,1)} %constant.4.clone.perm), custom_call_target="tpu_custom_call" | custom-call | tf_op jit(solution)/shard_map/pallas_call | solution.py:199
  70.1 0.0 copy-done
  70.1 2.3 %fusion = f32[256,512]{1,0:T(8,128)} fusion(f32[256,128]{1,0:T(8,128)S(1)} %copy-done, f32[128,512]{1,0:T(8,128)} %shard_map.37), kind=kOutput, calls=%fused_computation | convolution fusion | flops 201326592 | bytes 917504 | tf_op jit(solution)/shard_map/dot_general | solution.py:225
Async XLA Ops:
  0.0 70.1 %copy-start = (f32[256,128]{1,0:T(8,128)S(1)}, f32[256,128]{1,0:T(8,128)}, u32[]{:S(2)}) copy-start(f32[256,128]{1,0:T(8,128)} %constant.5.clone) | copy-start | bytes 393220
where the time goes:
time: 72.6 us; the launch traced here: 72.5 us
  Pallas kernels  70.1 us (97%)
  matrix products  2.32 us (3%)
    pallas_call x1, Pallas kernels, on_device(): pl.pallas_call(functools.partial(kernel, n, T, G, mj, iw), out_shape=jax....  70.1 us
    dot_general x1, matrix products, on_device(): jnp.dot(jnp.asarray(table, jnp.float32), lagged, preferred_element_type=j...  2.32 us

commit v1 on v0

--- a/solution.py
+++ b/solution.py
@@ -25,6 +25,31 @@
         out = out + ((b + (1 if mask & bit else 0)) % 2) * bit
         bit *= 2
     return out
+
+
+def code_levels(limit):
+    for m in range(8192, 128, -128):
+        steps = [m * e + limit / 2**e for e in range(20)]
+        if min(steps) <= 32700:
+            return m, int(np.argmin(steps)) + 1
+
+
+def encoded(value, m, levels):
+    size = jnp.abs(value)
+    code = size
+    for e in range(1, levels):
+        code = jnp.minimum(code, size * 0.5**e + float(m * e))
+    code = (code + 0.5).astype(jnp.int32)
+    return jnp.where(value < 0, -code, code).astype(jnp.int16)
+
+
+def decoded(code, m, levels):
+    code = code.astype(jnp.int32).astype(jnp.float32)
+    size = jnp.abs(code)
+    value = size
+    for e in range(1, levels):
+        value = jnp.maximum(value, (size - float(m * e)) * 2.0**e)
+    return jnp.where(code < 0, -value, value)
 
 
 def kernel(n, T, G, mj, iw, samples, perm, out, vbuf, ts, tb, ut, acc, sbuf, rbuf,
@@ -37,6 +62,8 @@
     rows = samples.shape[0]
     R = rows // Q
     C = G // 2
+    half = Q // 4
+    m_code, levels = code_levels(rows * G * 64)
 
     for q in range(Q):
         phase = samples[pl.ds(q, R, stride=Q), :].astype(jnp.float32).astype(jnp.bfloat16)
@@ -58,10 +85,11 @@
             src_ref=ts.at[d], dst_ref=tb.at[G], send_sem=send_h.at[d], recv_sem=recv_t.at[G],
             device_id=(base - G + d,), device_id_type=MESH)
 
-    def copy_v(slot, d, sem):
+    def copy_v(slot, d, h, sem):
+        part = vbuf.at[slot, pl.ds(h * half, half)]
         return pltpu.make_async_remote_copy(
-            src_ref=vbuf.at[slot], dst_ref=vbuf.at[slot], send_sem=send_v.at[sem],
-            recv_sem=recv_v.at[slot], device_id=(base + d,), device_id_type=MESH)
+            src_ref=part, dst_ref=part, send_sem=send_v.at[sem, h],
+            recv_sem=recv_v.at[slot, h], device_id=(base + d,), device_id_type=MESH)
 
     partner = flipped(g, 1)
     for k in range(1, G):
@@ -72,9 +100,23 @@
         for d in range(G):
             copy_h(d).start()
 
-    for c in range(1, C):
-        copy_v(g, flipped(g, 2 * c), c).start()
-    copy_v(g, partner, 0).start()
+    relay = C == 4
+    sends = []
+
+    def send(*what):
+        copy_v(*what).start()
+        sends.append(what)
+
+    if relay:
+        for k in range(2):
+            send(g, flipped(g, 2), 1 - k, 1)
+            send(g, flipped(g, 4), k, 2)
+    else:
+        for c in range(1, C):
+            for h in range(2):
+                send(g, flipped(g, 2 * c), h, c)
+    for h in range(2):
+        send(g, partner, h, 0)
 
     tb[g] = ts[g]
 
@@ -117,25 +159,55 @@
 
         lax.fori_loop(0, OUT_ROWS // TILE, tile, 0)
 
-    def wait_v(s):
-        pltpu.make_async_copy(vbuf.at[s], vbuf.at[s], recv_v.at[s]).wait()
+    def wait_v(s, h):
+        part = vbuf.at[s, pl.ds(h * half, half)]
+        pltpu.make_async_copy(part, part, recv_v.at[s, h]).wait()
+
+    def wait_both(s):
+        wait_v(s, 0)
+        wait_v(s, 1)
 
     multiply(g, True)
-    wait_v(partner)
+    wait_both(partner)
     multiply(partner, False)
-    for c in range(1, C):
-        s = flipped(g, 2 * c)
-        wait_v(s)
-        copy_v(s, partner, C + c - 1).start()
-        multiply(s, False)
-        if c > 1:
-            s2 = flipped(g, 2 * (c - 1) + 1)
-            wait_v(s2)
+    if relay:
+        x, y, z = (flipped(g, mask) for mask in (2, 4, 6))
+        wait_v(x, 1)
+        send(x, y, 1, 3)
+        wait_v(y, 0)
+        send(y, x, 0, 3)
+        send(x, partner, 1, 4)
+        send(y, partner, 0, 5)
+        wait_v(x, 0)
+        send(x, partner, 0, 4)
+        wait_v(y, 1)
+        send(y, partner, 1, 5)
+        multiply(x, False)
+        multiply(y, False)
+        for mask in (3, 5):
+            wait_both(flipped(g, mask))
+            multiply(flipped(g, mask), False)
+        for h in range(2):
+            wait_v(z, h)
+            send(z, partner, h, 6)
+        multiply(z, False)
+        wait_both(flipped(g, 7))
+        multiply(flipped(g, 7), False)
+    else:
+        for c in range(1, C):
+            s = flipped(g, 2 * c)
+            for h in range(2):
+                wait_v(s, h)
+                send(s, partner, h, C + c - 1)
+            multiply(s, False)
+            if c > 1:
+                s2 = flipped(g, 2 * (c - 1) + 1)
+                wait_both(s2)
+                multiply(s2, False)
+        if C > 1:
+            s2 = flipped(g, 2 * (C - 1) + 1)
+            wait_both(s2)
             multiply(s2, False)
-    if C > 1:
-        s2 = flipped(g, 2 * (C - 1) + 1)
-        wait_v(s2)
-        multiply(s2, False)
 
     def piece(j):
         full = acc[0, pl.ds(j, LAGS, stride=JS), :] + acc[1, pl.ds(JS + j, LAGS, stride=JS), :]
@@ -153,19 +225,16 @@
         d = (t + k) % T
         for m in range(mj):
             if k:
-                sbuf[d, m] = piece(d * mj + m)
+                sbuf[d, m] = encoded(piece(d * mj + m), m_code, levels)
             else:
-                rbuf[t, m] = piece(d * mj + m)
+                out[:, m * iw:(m + 1) * iw] = piece(d * mj + m)
         if k:
             copy_r(k).start()
     for k in range(1, T):
         s = (t + T - k) % T
         pltpu.make_async_copy(rbuf.at[s], rbuf.at[s], recv_r.at[s]).wait()
-    for m in range(mj):
-        total = rbuf[0, m]
-        for k in range(1, T):
-            total = total + rbuf[k, m]
-        out[:, m * iw:(m + 1) * iw] = total
+        for m in range(mj):
+            out[:, m * iw:(m + 1) * iw] += decoded(rbuf[s, m], m_code, levels)
 
     for k in range(1, G):
         copy_t(k).wait_send()
@@ -175,10 +244,8 @@
         for d in range(G):
             copy_h(d).wait_send()
 
-    for c in range(1, C):
-        copy_v(g, flipped(g, 2 * c), c).wait_send()
-        copy_v(flipped(g, 2 * c), partner, C + c - 1).wait_send()
-    copy_v(g, partner, 0).wait_send()
+    for what in sends:
+        copy_v(*what).wait_send()
     for k in range(1, T):
         copy_r(k).wait_send()
 
@@ -207,10 +274,10 @@
             pltpu.VMEM((G + 1, Q * JS, R), jnp.bfloat16),
             pltpu.VMEM((G, TAUS * JS, R), jnp.bfloat16),
             pltpu.VMEM((2, OUT_ROWS, width), jnp.float32),
-            pltpu.VMEM((T, mj, LAGS, iw), jnp.float32),
-            pltpu.VMEM((T, mj, LAGS, iw), jnp.float32),
-            pltpu.SemaphoreType.DMA((G,)),
-            pltpu.SemaphoreType.DMA((G,)),
+            pltpu.VMEM((T, mj, LAGS, iw), jnp.int16),
+            pltpu.VMEM((T, mj, LAGS, iw), jnp.int16),
+            pltpu.SemaphoreType.DMA((G, 2)),
+            pltpu.SemaphoreType.DMA((G, 2)),
             pltpu.SemaphoreType.DMA((G,)),
             pltpu.SemaphoreType.DMA((G + 1,)),
             pltpu.SemaphoreType.DMA((G,)),

time: 72.6 us -> 56.8 us (0.78)
  Pallas kernels: 70.1 us -> 54.1 us
    pallas_call x1, Pallas kernels: 70.1 us -> 54.1 us  [on_device(): pl.pallas_call(functools.partial(kernel, n, T, G, mj, iw), out_shape=jax....]
where the time goes in v1:
time: 56.8 us; the launch traced here: 56.4 us
  Pallas kernels  54.1 us (95%)
  matrix products  2.31 us (4%)
    pallas_call x1, Pallas kernels, on_device(): pl.pallas_call(functools.partial(kernel, n, T, G, mj, iw), out_shape=jax....  54.1 us
    dot_general x1, matrix products, on_device(): jnp.dot(jnp.asarray(table, jnp.float32), lagged, preferred_element_type=j...  2.31 us

profile of v1, /device:TPU:8, one launch (start us, length us, event | category | flops | bytes accessed | tf_op | source)
XLA Modules:
  0.0 56.4 jit_solution(10255862641990416432)
XLA Ops:
  0.0 0.0 copy-start
  0.0 54.1 %shard_map.37 = f32[128,512]{1,0:T(8,128)} custom-call(s32[2048,128]{1,0:T(8,128)} %samples.1, bf16[128,128]{1,0:T(8,128)(2,1)} %constant.4.clone.perm), custom_call_target="tpu_custom_call" | custom-call | tf_op jit(solution)/shard_map/pallas_call | solution.py:266
  54.1 0.0 copy-done
  54.1 2.3 %fusion = f32[256,512]{1,0:T(8,128)} fusion(f32[256,128]{1,0:T(8,128)S(1)} %copy-done, f32[128,512]{1,0:T(8,128)} %shard_map.37), kind=kOutput, calls=%fused_computation | convolution fusion | flops 201326592 | bytes 917504 | tf_op jit(solution)/shard_map/dot_general | solution.py:292
Async XLA Ops:
  0.0 54.1 %copy-start = (f32[256,128]{1,0:T(8,128)S(1)}, f32[256,128]{1,0:T(8,128)}, u32[]{:S(2)}) copy-start(f32[256,128]{1,0:T(8,128)} %constant.5.clone) | copy-start | bytes 393220

commit v2 on v1

--- a/solution.py
+++ b/solution.py
@@ -65,14 +65,26 @@
     half = Q // 4
     m_code, levels = code_levels(rows * G * 64)
 
+    barrier = pltpu.get_barrier_semaphore()
+
+    def greet(device):
+        pl.semaphore_signal(barrier, inc=1, device_id=(device,), device_id_type=MESH)
+
+    for k in range(1, G):
+        greet(base + flipped(g, k))
+    for k in range(1, T):
+        greet((t + k) % T * G + g)
+
+    @pl.when(t < T - 1)
+    def _():
+        greet(base + G)
+
     for q in range(Q):
         phase = samples[pl.ds(q, R, stride=Q), :].astype(jnp.float32).astype(jnp.bfloat16)
         vbuf[g, q // 2, :, (q % 2) * 128:(q % 2 + 1) * 128] = phase
-        turned = lax.dot_general(
-            perm[...], phase, (((1,), (1,)), ((), ())), preferred_element_type=jnp.float32
-        ).astype(jnp.bfloat16)
-        for d in range(G):
-            ts[d, q * JS:(q + 1) * JS, :] = turned[d * JS:(d + 1) * JS, :]
+
+    feeds = jnp.logical_and(g == 0, t > 0)
+    pl.semaphore_wait(barrier, jnp.where(feeds, 2 * G + T - 2, G + T - 2))
 
     def copy_t(k):
         d = flipped(g, k)
@@ -92,14 +104,6 @@
             recv_sem=recv_v.at[slot, h], device_id=(base + d,), device_id_type=MESH)
 
     partner = flipped(g, 1)
-    for k in range(1, G):
-        copy_t(k).start()
-
-    @pl.when(jnp.logical_and(g == 0, t > 0))
-    def _():
-        for d in range(G):
-            copy_h(d).start()
-
     relay = C == 4
     sends = []
 
@@ -108,9 +112,28 @@
         sends.append(what)
 
     if relay:
-        for k in range(2):
-            send(g, flipped(g, 2), 1 - k, 1)
-            send(g, flipped(g, 4), k, 2)
+        send(g, flipped(g, 2), 1, 1)
+        send(g, flipped(g, 4), 0, 2)
+
+    for q in range(Q):
+        turned = lax.dot_general(
+            perm[...], vbuf[g, q // 2, :, (q % 2) * 128:(q % 2 + 1) * 128],
+            (((1,), (1,)), ((), ())), preferred_element_type=jnp.float32
+        ).astype(jnp.bfloat16)
+        for d in range(G):
+            ts[d, q * JS:(q + 1) * JS, :] = turned[d * JS:(d + 1) * JS, :]
+
+    for k in range(G - 1, 0, -1):
+        copy_t(k).start()
+
+    @pl.when(jnp.logical_and(g == 0, t > 0))
+    def _():
+        for d in range(G):
+            copy_h(d).start()
+
+    if relay:
+        send(g, flipped(g, 2), 0, 1)
+        send(g, flipped(g, 4), 1, 2)
     else:
         for c in range(1, C):
             for h in range(2):
@@ -284,14 +307,14 @@
             pltpu.SemaphoreType.DMA((T,)),
             pltpu.SemaphoreType.DMA((T,)),
         ],
-        compiler_params=pltpu.CompilerParams(has_side_effects=True, vmem_limit_bytes=56 * 1024 * 1024),
+        compiler_params=pltpu.CompilerParams(has_side_effects=True, collective_id=0, vmem_limit_bytes=56 * 1024 * 1024),
     )(samples, jnp.asarray(perm, jnp.bfloat16))
     k = np.arange(LAGS)
     angle = 2.0 * np.pi / LAGS * (np.outer(k, k) % LAGS)
     table = np.concatenate([np.cos(angle), -np.sin(angle)]) / (16.0 * rows * n)
     spectra = jnp.dot(
         jnp.asarray(table, jnp.float32), lagged,
-        preferred_element_type=jnp.float32, precision=lax.Precision.HIGHEST)
+        preferred_element_type=jnp.float32, precision=lax.Precision.HIGH)
     return spectra.reshape(2, LAGS, owned)
 
 

time: 56.8 us -> 53 us (0.933)
  Pallas kernels: 54.1 us -> 50.1 us
    pallas_call x1, Pallas kernels: 54.1 us -> 50.1 us  [on_device(): pl.pallas_call(functools.partial(kernel, n, T, G, mj, iw), out_shape=jax....]
where the time goes in v2:
time: 53 us; the launch traced here: 52.2 us
  Pallas kernels  50.1 us (95%)
  matrix products  2.1 us (4%)
    pallas_call x1, Pallas kernels, on_device(): pl.pallas_call(functools.partial(kernel, n, T, G, mj, iw), out_shape=jax....  50.1 us
    dot_general x1, matrix products, on_device(): jnp.dot(jnp.asarray(table, jnp.float32), lagged, preferred_element_type=j...  2.1 us

profile of v2, /device:TPU:8, one launch (start us, length us, event | category | flops | bytes accessed | tf_op | source)
XLA Modules:
  0.0 52.2 jit_solution(11530093996007899473)
XLA Ops:
  0.0 0.0 copy-start
  0.0 50.1 %shard_map.37 = f32[128,512]{1,0:T(8,128)} custom-call(s32[2048,128]{1,0:T(8,128)} %samples.1, bf16[128,128]{1,0:T(8,128)(2,1)} %constant.4.clone.perm), custom_call_target="tpu_custom_call" | custom-call | tf_op jit(solution)/shard_map/pallas_call | solution.py:289
  50.1 0.0 copy-done
  50.1 2.1 %fusion = f32[256,512]{1,0:T(8,128)} fusion(f32[256,128]{1,0:T(8,128)S(1)} %copy-done, f32[128,512]{1,0:T(8,128)} %shard_map.37), kind=kOutput, calls=%fused_computation | convolution fusion | flops 100663296 | bytes 917504 | tf_op jit(solution)/shard_map/dot_general | solution.py:315
Async XLA Ops:
  0.0 50.1 %copy-start = (f32[256,128]{1,0:T(8,128)S(1)}, f32[256,128]{1,0:T(8,128)}, u32[]{:S(2)}) copy-start(f32[256,128]{1,0:T(8,128)} %constant.5.clone) | copy-start | bytes 393220
